TPU v7x, 32 devices: a whole 2x2x4 slice. The times are simulated.
32 devices in a mesh: tm: 8 (over y, x, core), batch: 4 (over z).
Axes of the slice: x: 2, y: 2, z: 4, core: 2. Of those that a mesh axis runs over, the one named last changes fastest.
Arguments:
- hidden_states: bfloat16 [4, 1024, 5120], P('batch', 'tm'), may hold values from -6 to 6
- gen_weight: bfloat16 [64, 5120], replicated, may hold values from -0.078125 to 0.078125
- noise_field: bfloat16 [4, 64, 1024], P('batch', None, 'tm'), may hold values from -6 to 6
- timesteps: int32 [4], P('batch'), may hold values from 200 to 999
- embed_real: bfloat16 [128, 5120], replicated, may hold values from -0.5 to 0.5
- time_real: bfloat16 [256, 3, 5120], P('tm'), may hold values from -0.375 to 0.375
- query_real: bfloat16 [5120, 1024], P(None, 'tm'), may hold values from -3 to 3
- key_real: bfloat16 [5120, 1024], P(None, 'tm'), may hold values from -3 to 3
- value_real: bfloat16 [5120, 1024], P(None, 'tm'), may hold values from -0.078125 to 0.078125
- out_real: bfloat16 [1024, 5120], P('tm'), may hold values from -0.1875 to 0.1875
- gain_real: float32 [2, 1024], P(None, 'tm'), may hold values from 0.25 to 3
- proj_real: bfloat16 [64, 5120], replicated, may hold values from -0.078125 to 0.078125
- embed_fake: bfloat16 [128, 5120], replicated, may hold values from -0.5 to 0.5
- time_fake: bfloat16 [256, 3, 5120], P('tm'), may hold values from -0.375 to 0.375
- query_fake: bfloat16 [5120, 1024], P(None, 'tm'), may hold values from -3 to 3
- key_fake: bfloat16 [5120, 1024], P(None, 'tm'), may hold values from -3 to 3
- value_fake: bfloat16 [5120, 1024], P(None, 'tm'), may hold values from -0.078125 to 0.078125
- out_fake: bfloat16 [1024, 5120], P('tm'), may hold values from -0.1875 to 0.1875
- gain_fake: float32 [2, 1024], P(None, 'tm'), may hold values from 0.25 to 3
- proj_fake: bfloat16 [64, 5120], replicated, may hold values from -0.078125 to 0.078125
Outputs:
- dmd_gradient: float32 [4, 64, 1024], P('batch', None, 'tm')
- weight_grad: float32 [64, 5120], replicated
All inputs are finite; a program needn't handle non-finite values.
Results may differ from a plain program's by a relative error of at most 0.019.
Values may be sent and summed in bfloat16 or wider, within the bound.
A program may use at most 128 MiB of HBM per device.

v0:
```python
import math
import jax
import jax.numpy as jnp
from jax import lax
from jax.sharding import PartitionSpec as P

HD = 128
FREQ = 256
FTOK = 128
norm_floor = 0.05
gap_floor = 0.25
highest = lax.Precision.HIGHEST


def from_behind(shard, axis, by):
    size = lax.axis_size(axis)
    pairs = [(i, i + by) for i in range(size) if 0 <= i + by < size]
    return lax.ppermute(shard, axis, pairs)


def sinusoid(time_step):
    half_freq = FREQ // 2
    frequency = jnp.exp(-math.log(10000.0) * jnp.arange(half_freq, dtype=jnp.float32) / half_freq)
    angles = time_step.astype(jnp.float32) * frequency
    return jnp.concatenate([jnp.cos(angles), jnp.sin(angles)]).astype(jnp.bfloat16)


def embed_stats(stacked, embed_table):
    embedded = lax.dot_general(
        stacked, embed_table, (((0,), (0,)), ((), ())), preferred_element_type=jnp.float32
    )
    row_mean = jnp.mean(embedded, axis=1)
    centered = embedded - row_mean[:, None]
    rscale = lax.rsqrt(jnp.mean(centered * centered, axis=1) + norm_floor)
    return (embedded, row_mean, rscale)


def fold_heads(embed_table, modulation, query_proj, key_proj, value_proj):
    scale_row = 1.0 + modulation[1]
    widened = embed_table.astype(jnp.float32) * scale_row[None, :]

    def fold_one(weight):
        wide_weight = weight.astype(jnp.float32)
        main_part = jnp.dot(widened, wide_weight, precision=highest)
        column_sum = jnp.dot(scale_row, wide_weight, precision=highest)
        offset = jnp.dot(modulation[0], wide_weight, precision=highest)
        return jnp.concatenate([main_part, column_sum[None, :], offset[None, :]], axis=0)

    return jnp.stack([fold_one(query_proj), fold_one(key_proj), fold_one(value_proj)])


def project(stacked, row_mean, rscale, folded):
    kin_rows = stacked.shape[0]
    base_part = jnp.einsum(
        "kr,pkc->prc", stacked.astype(jnp.float32), folded[:, :kin_rows], precision=highest
    )
    return (
        rscale[None, :, None] * base_part
        - (rscale * row_mean)[None, :, None] * folded[:, kin_rows][:, None, :]
        + folded[:, kin_rows + 1][:, None, :]
    )


def rms_round(vector, total_sq, columns, gain_row):
    return (
        vector * lax.rsqrt(total_sq / columns + norm_floor)[:, None] * gain_row[None, :]
    ).astype(jnp.bfloat16)


def attend(query_norm, key_norm, value_norm):
    token_count = query_norm.shape[0]
    block_rows = min(512, token_count)
    frames = jnp.arange(token_count, dtype=jnp.int32) // FTOK

    def one_block(row_start):
        query_block = lax.dynamic_slice_in_dim(query_norm, row_start, block_rows, 0)
        scores = jnp.einsum(
            "qhd,khd->hqk", query_block, key_norm, preferred_element_type=jnp.float32
        ) / math.sqrt(HD)
        query_frames = lax.dynamic_slice_in_dim(frames, row_start, block_rows, 0)
        allowed = frames[None, :] <= query_frames[:, None]
        scores = jnp.where(allowed[None], scores, -1e30)
        row_peak = jnp.max(scores, axis=2, keepdims=True)
        exp_scores = jnp.exp(scores - row_peak)
        attn_probs = (exp_scores / jnp.sum(exp_scores, axis=2, keepdims=True)).astype(jnp.bfloat16)
        return jnp.einsum(
            "hqk,khd->qhd", attn_probs, value_norm, preferred_element_type=jnp.float32
        ).astype(jnp.bfloat16)

    starts = jnp.arange(token_count // block_rows, dtype=jnp.int32) * block_rows
    pieces = lax.map(one_block, starts)
    return pieces.reshape(token_count, query_norm.shape[1], query_norm.shape[2])


def head_terms(attended, out_rows, modulation, final_proj):
    gated = out_rows.astype(jnp.float32) * modulation[2][None, :]
    folded_out = lax.dot_general(
        gated, final_proj.astype(jnp.float32), (((1,), (1,)), ((), ())), precision=highest
    )
    flat_heads = attended.reshape(attended.shape[0], -1).astype(jnp.float32)
    return lax.dot_general(folded_out, flat_heads, (((0,), (1,)), ((), ())), precision=highest)


def per_device(
    hidden_states,
    gen_weight,
    noise_field,
    timesteps,
    embed_real,
    time_real,
    query_real,
    key_real,
    value_real,
    out_real,
    gain_real,
    proj_real,
    embed_fake,
    time_fake,
    query_fake,
    key_fake,
    value_fake,
    out_fake,
    gain_fake,
    proj_fake,
):
    devices = lax.axis_size("tm")
    frame_tokens = hidden_states.shape[1]
    tokens = frame_tokens * devices
    patch_rows = gen_weight.shape[0]
    time_step = timesteps[0]
    level_raw = time_step.astype(jnp.float32) / 1000.0
    noise_level = 5.0 * level_raw / (1.0 + 4.0 * level_raw)
    generated = lax.dot_general(
        gen_weight, hidden_states[0], (((1,), (1,)), ((), ())), preferred_element_type=jnp.float32
    ).astype(jnp.bfloat16)
    noisy_patch = (
        (1.0 - noise_level) * generated.astype(jnp.float32)
        + noise_level * noise_field[0].astype(jnp.float32)
    ).astype(jnp.bfloat16)
    sinus_wave = sinusoid(time_step)
    freq_rows = time_real.shape[0]
    own_wave = lax.dynamic_slice_in_dim(sinus_wave, lax.axis_index("tm") * freq_rows, freq_rows, 0)
    share_real = jnp.einsum("f,fcd->cd", own_wave, time_real, preferred_element_type=jnp.float32)
    share_fake = jnp.einsum("f,fcd->cd", own_wave, time_fake, preferred_element_type=jnp.float32)
    modul_real, modul_fake = lax.psum((share_real, share_fake), "tm")
    earlier = from_behind(noisy_patch, "tm", 1)
    stacked = jnp.concatenate([noisy_patch, earlier], axis=0)
    embedded_real, mean_real, rscale_real = embed_stats(stacked, embed_real)
    embedded_fake, mean_fake, rscale_fake = embed_stats(stacked, embed_fake)
    folded_real = fold_heads(embed_real, modul_real, query_real, key_real, value_real)
    folded_fake = fold_heads(embed_fake, modul_fake, query_fake, key_fake, value_fake)
    local_width = query_real.shape[1]
    local_heads = local_width // HD
    columns = local_width * devices
    gathered = (
        lax.all_gather(noisy_patch.astype(jnp.float32), "tm", axis=1, tiled=True),
        lax.all_gather(mean_real, "tm", axis=0, tiled=True),
        lax.all_gather(rscale_real, "tm", axis=0, tiled=True),
        lax.all_gather(mean_fake, "tm", axis=0, tiled=True),
        lax.all_gather(rscale_fake, "tm", axis=0, tiled=True),
    )
    all_patch = gathered[0].astype(jnp.bfloat16)
    prior_frame = jnp.concatenate(
        [
            jnp.zeros((patch_rows, frame_tokens), jnp.bfloat16),
            all_patch[:, : tokens - frame_tokens],
        ],
        axis=1,
    )
    all_stacked = jnp.concatenate([all_patch, prior_frame], axis=0)
    qkv_real = project(all_stacked, gathered[1], gathered[2], folded_real)
    qkv_fake = project(all_stacked, gathered[3], gathered[4], folded_fake)
    norm_sums = lax.psum(
        (
            jnp.sum(qkv_real[0] * qkv_real[0], axis=1),
            jnp.sum(qkv_real[1] * qkv_real[1], axis=1),
            jnp.sum(qkv_fake[0] * qkv_fake[0], axis=1),
            jnp.sum(qkv_fake[1] * qkv_fake[1], axis=1),
        ),
        "tm",
    )
    head_shape = (tokens, local_heads, HD)
    attended_real = attend(
        rms_round(qkv_real[0], norm_sums[0], columns, gain_real[0]).reshape(head_shape),
        rms_round(qkv_real[1], norm_sums[1], columns, gain_real[1]).reshape(head_shape),
        qkv_real[2].astype(jnp.bfloat16).reshape(head_shape),
    )
    attended_fake = attend(
        rms_round(qkv_fake[0], norm_sums[2], columns, gain_fake[0]).reshape(head_shape),
        rms_round(qkv_fake[1], norm_sums[3], columns, gain_fake[1]).reshape(head_shape),
        qkv_fake[2].astype(jnp.bfloat16).reshape(head_shape),
    )
    term_real = head_terms(attended_real, out_real, modul_real, proj_real)
    term_fake = head_terms(attended_fake, out_fake, modul_fake, proj_fake)
    own_real, own_fake = (
        lax.psum_scatter(term_real, "tm", scatter_dimension=1, tiled=True),
        lax.psum_scatter(term_fake, "tm", scatter_dimension=1, tiled=True),
    )
    velocity_real = own_real + lax.dot_general(
        proj_real.astype(jnp.float32), embedded_real, (((1,), (1,)), ((), ())), precision=highest
    )
    velocity_fake = own_fake + lax.dot_general(
        proj_fake.astype(jnp.float32), embedded_fake, (((1,), (1,)), ((), ())), precision=highest
    )
    pred_real = noisy_patch.astype(jnp.float32) - noise_level * velocity_real
    pred_fake = noisy_patch.astype(jnp.float32) - noise_level * velocity_fake
    gap_local = jnp.sum(jnp.abs(generated.astype(jnp.float32) - pred_real))
    count_all = patch_rows * tokens
    grad_root = math.sqrt(lax.axis_size("batch") * hidden_states.shape[0] * tokens)
    gap_diff = pred_fake - pred_real
    difference = gap_diff.astype(jnp.bfloat16)
    partial_grad = jnp.dot(difference, hidden_states[0], preferred_element_type=jnp.float32)
    gap_total = lax.psum(gap_local, "tm")
    normalizer = jnp.maximum(gap_total / count_all, gap_floor)
    weight_grad = lax.psum(partial_grad / normalizer / grad_root, ("tm", "batch"))
    dmd_gradient = (gap_diff / normalizer)[None]
    return (dmd_gradient, weight_grad)


def solution(mesh):
    in_specs = (
        P("batch", "tm", None),
        P(),
        P("batch", None, "tm"),
        P("batch"),
        P(),
        P("tm", None, None),
        P(None, "tm"),
        P(None, "tm"),
        P(None, "tm"),
        P("tm", None),
        P(None, "tm"),
        P(),
        P(),
        P("tm", None, None),
        P(None, "tm"),
        P(None, "tm"),
        P(None, "tm"),
        P("tm", None),
        P(None, "tm"),
        P(),
    )
    out_specs = (P("batch", None, "tm"), P())
    return jax.shard_map(
        per_device, mesh=mesh, in_specs=in_specs, out_specs=out_specs, check_vma=False
    )
```

profile of v0, /device:TPU:0, one launch (start us, length us, event | category | flops | bytes accessed | tf_op | source)
XLA Modules:
  0.0 419.4 jit_solution(4317178082355693844)
XLA Ops:
  8.5 2.4 fusion.74
  10.9 2.4 collective-permute-start
  16.0 25.7 %psum.59 = f32[3,5120]{1,0:T(4,128)S(1)} all-reduce(f32[3,5120]{1,0:T(4,128)S(1)} %bitcast.296), channel_id=1, replica_groups=mesh['tm'=8,'batch'=4] {'tm'}, use_global_device_ids=true, to_apply=%region_12.0 | all-reduce | flops 15360 | bytes 122880 | tf_op jit(solution)/shard_map/psum | solution.py:145
  54.8 3.7 fusion.20
  58.5 10.2 %all_gather.16 = bf16[64,1024]{1,0:T(8,128)(2,1)S(1)} all-gather(bf16[64,128]{1,0:T(8,128)(2,1)S(1)} %get-tuple-element.224), channel_id=1, replica_groups=mesh['tm'=8,'batch'=4] {'tm'}, dimensions={1}, use_global_device_ids=true | all-gather | bytes 147456 | tf_op jit(solution)/shard_map/all_gather | solution.py:156
  70.5 7.6 %all-gather.2 = f32[8,1,128]{2,1,0:T(1,128)S(1)} all-gather(f32[1,1,128]{2,1,0:T(1,128)S(1)} %rsqrt_bitcast_fusion), channel_id=1, replica_groups=mesh['tm'=8,'batch'=4] {'tm'}, dimensions={0}, use_global_device_ids=true | all-gather | bytes 4608 | tf_op jit(solution)/shard_map/all_gather | solution.py:158
  78.1 9.0 %all-gather.3 = f32[8,1,128]{2,1,0:T(1,128)S(1)} all-gather(f32[1,1,128]{2,1,0:T(1,128)S(1)} %get-tuple-element.222), channel_id=1, replica_groups=mesh['tm'=8,'batch'=4] {'tm'}, dimensions={0}, use_global_device_ids=true | all-gather | bytes 4608 | tf_op jit(solution)/shard_map/all_gather | solution.py:157
  94.5 7.9 %all-gather = f32[8,1,128]{2,1,0:T(1,128)S(1)} all-gather(f32[1,1,128]{2,1,0:T(1,128)} %rsqrt_bitcast_fusion.1), channel_id=1, replica_groups=mesh['tm'=8,'batch'=4] {'tm'}, dimensions={0}, use_global_device_ids=true | all-gather | bytes 4608 | tf_op jit(solution)/shard_map/all_gather | solution.py:160
  102.4 8.7 %all-gather.1 = f32[8,1,128]{2,1,0:T(1,128)S(1)} all-gather(f32[1,1,128]{2,1,0:T(1,128)} %get-tuple-element.220), channel_id=1, replica_groups=mesh['tm'=8,'batch'=4] {'tm'}, dimensions={0}, use_global_device_ids=true | all-gather | bytes 4608 | tf_op jit(solution)/shard_map/all_gather | solution.py:159
  111.7 33.1 %all-reduce.8.cloned.1.call-done = (f32[1024]{0:T(1024)}, f32[1024]{0:T(1024)}, f32[3,5120]{1,0:T(4,128)}) async-done(((f32[1024]{0:T(1024)}, f32[1024]{0:T(1024)}, f32[3,5120]{1,0:T(4,128)}), (f32[1024]{0:T(1024)}, f32[1024]{0:T(1024)}, f32[3,5120]{1,0:T(4,128)})) %all-reduce.8.cloned.1.call-update) | async-done | bytes 69648 | tf_op jit(solution)/shard_map/psum | solution.py:173
  146.5 2.0 fusion.93
  148.4 2.0 fusion.83
  158.9 9.1 %while.23 = (s32[]{:T(128)}, bf16[2,512,1,128]{3,1,2,0:T(8,128)(2,1)S(1)}, s32[1024]{0:T(1024)S(1)}, s32[2]{0:T(128)S(1)}, bf16[1024,1,128]{0,2,1:T(8,128)(2,1)S...) while((s32[]{:T(128)}, ...), condition=%wide.region_22.23_spmd.clone, body=%wide.region_19.22_spmd.clone.sunk | while | flops 273218560 | bytes 7098535 | solution.py:91
  169.4 2.1 fusion.30
  172.2 1.8 copy.41
  174.7 3.9 fusion.26
  178.6 25.1 %reduce-scatter.5.cloned.1.call-done = f32[64,128]{1,0:T(8,128)} async-done(((f32[64,1024]{1,0:T(8,128)}), f32[64,128]{1,0:T(8,128)}) %reduce-scatter.5.cloned.1.call-update) | async-done | bytes 32784 | tf_op jit(solution)/shard_map/reduce_scatter | solution.py:196
  203.6 4.6 %abs_reduce_fusion = (f32[]{:T(128)}, f32[64,128]{1,0:T(8,128)}) fusion(f32[64,128]{1,0:T(8,128)} %get-tuple-element.225, f32[64,128]{1,0:T(8,128)} %reduce-scatter.5.cloned.1.call-done, f32[128,5120]{1,0:T(8,128)} %copy-done.2, bf16[64,5120]{1,0:T(8,128)(2,1)S(1)} %copy-done.15, f32[]{:T(128)S(6)} %div.95, bf16[64,128]{1,0:T(8,128)(2,1)S(1)} %get-tuple-element.224), kind=kOutput, calls=%fused_computation.110 | convolution fusion | flops 503373824 | bytes 3391496 | tf_op jit(solution)/shard_map/dot_general | solution.py:199
  208.3 13.3 %all-reduce.1 = (f32[1024]{0:T(1024)S(1)}, f32[1024]{0:T(1024)S(1)}, f32[]{:T(128)}) all-reduce(f32[1024]{0:T(1024)} %get-tuple-element.163, f32[1024]{0:T(1024)} %get-tuple-element.162, f32[]{:T(128)} %get-tuple-element.230), channel_id=1, replica_groups=mesh['tm'=8,'batch'=4] {'tm'}, use_global_device_ids=true, to_apply=%region_4.0 | all-reduce | flops 2049 | bytes 16392 | tf_op jit(solution)/shard_map/psum | solution.py:173
  223.3 14.2 %while.22 = (s32[]{:T(128)}, bf16[2,512,1,128]{3,1,2,0:T(8,128)(2,1)S(1)}, s32[1024]{0:T(1024)}, s32[2]{0:T(128)}, bf16[1024,1,128]{0,2,1:T(8,128)(2,1)}, /*inde...) while((s32[]{:T(128)}, ...), condition=%wide.region_10.0_spmd.clone, body=%wide.region_7.10_spmd.clone.sunk | while | flops 273218560 | bytes 8147139 | solution.py:91
  239.3 33.3 %reduce-scatter.3.cloned.1.call-done = f32[64,128]{1,0:T(8,128)} async-done(((f32[64,1024]{1,0:T(8,128)}), f32[64,128]{1,0:T(8,128)}) %reduce-scatter.3.cloned.1.call-update) | async-done | bytes 32784 | tf_op jit(solution)/shard_map/reduce_scatter | solution.py:197
  272.6 3.4 fusion.46
  278.0 132.3 %all-reduce.6.cloned.1.call-done = f32[64,5120]{1,0:T(8,128)} async-done(((f32[64,5120]{1,0:T(8,128)}), f32[64,5120]{1,0:T(8,128)}) %all-reduce.6.cloned.1.call-update) | async-done | bytes 1310736 | tf_op jit(solution)/shard_map/psum | solution.py:215
  410.4 2.5 copy.87
  (176 shorter events, 59.2 us)
Async XLA Ops:
  7.2 137.6 %all-reduce.8.cloned.1.call-start = ((), (), s32[]{:S(2)}) async-start(), calls=%async_computation.5 | async-start | bytes 180224 | tf_op jit(solution)/shard_map/psum | solution.py:173
  8.5 33.3 %copy-start.5 = (bf16[5120,128]{1,0:T(8,128)(2,1)S(1)}, bf16[5120,128]{1,0:T(8,128)(2,1)}, u32[]{:S(2)}) copy-start(bf16[5120,128]{1,0:T(8,128)(2,1)} %param.32) | copy-start | bytes 3932164
  10.9 58.6 %collective-permute-start = (bf16[64,128]{1,0:T(8,128)(2,1)S(1)}, bf16[64,128]{1,0:T(8,128)(2,1)S(1)}, u32[]{:S(2)}, u32[]{:S(2)}) collective-permute-start(bf16[64,128]{1,0:T(8,128)(2,1)S(1)} %get-tuple-element.224), channel_id=1, source_target_pairs={{0,4},{4,8},{8,12},{12,16},{16,20},{20,24},{24,28},{1,5},{5,9},{9,... | collective-permute-start | bytes 49160 | tf_op jit(solution)/shard_map/ppermute | solution.py:18
  14.4 28.6 %copy-start.31 = (bf16[256]{0:T(256)(128)(2,1)}, bf16[256]{0:T(256)(128)(2,1)S(1)}, u32[]{:S(2)}) copy-start(bf16[256]{0:T(256)(128)(2,1)S(1)} %pad_maximum_fusion.9) | copy-start | bytes 1540
  50.6 3.6 copy-start.34
  50.6 4.2 %copy-start.15 = (bf16[64,5120]{1,0:T(8,128)(2,1)S(1)}, bf16[64,5120]{1,0:T(8,128)(2,1)}, u32[]{:S(2)}) copy-start(bf16[64,5120]{1,0:T(8,128)(2,1)} %param.35) | copy-start | bytes 1966084
  68.7 18.4 %copy-start.17 = (bf16[64,1024]{1,0:T(8,128)(2,1)}, bf16[64,1024]{1,0:T(8,128)(2,1)S(1)}, u32[]{:S(2)}) copy-start(bf16[64,1024]{1,0:T(8,128)(2,1)S(1)} %all_gather.16) | copy-start | bytes 393220
  68.7 18.4 %copy-start.25 = (bf16[64,896]{1,0:T(8,128)(2,1)}, bf16[64,896]{1,0:T(8,128)(2,1)S(1)}, u32[]{:S(2)}) copy-start(bf16[64,896]{1,0:T(8,128)(2,1)S(1)} %slice.122) | copy-start | bytes 344068
  70.1 18.1 %copy-start.2 = (f32[128,5120]{1,0:T(8,128)}, f32[128,5120]{1,0:T(8,128)S(1)}, u32[]{:S(2)}) copy-start(f32[128,5120]{1,0:T(8,128)S(1)} %get-tuple-element.227) | copy-start | bytes 7864324
  70.1 17.0 %copy-start.20 = (f32[3,130,128]{2,1,0:T(8,128)S(1)}, f32[3,130,128]{2,1,0:T(8,128)}, u32[]{:S(2)}) copy-start(f32[3,130,128]{2,1,0:T(8,128)} %pad_maximum_fusion.1) | copy-start | bytes 599044
  92.4 111.2 %reduce-scatter.5.cloned.1.call-start = ((), (), s32[]{:S(2)}) async-start(), calls=%async_computation.3 | async-start | bytes 294912 | tf_op jit(solution)/shard_map/reduce_scatter | solution.py:196
  102.4 42.3 %copy-start.28 = (f32[8,1,128]{2,1,0:T(1,128)}, f32[8,1,128]{2,1,0:T(1,128)S(1)}, u32[]{:S(2)}) copy-start(f32[8,1,128]{2,1,0:T(1,128)S(1)} %all-gather) | copy-start | bytes 12292
  144.8 5.7 %copy-start.10 = (bf16[5120,128]{1,0:T(8,128)(2,1)S(1)}, bf16[5120,128]{1,0:T(8,128)(2,1)}, u32[]{:S(2)}) copy-start(bf16[5120,128]{1,0:T(8,128)(2,1)} %param.39) | copy-start | bytes 3932164
  144.8 5.7 %copy-start.14 = (f32[3,5120]{1,0:T(4,128)S(1)}, f32[3,5120]{1,0:T(4,128)}, u32[]{:S(2)}) copy-start(f32[3,5120]{1,0:T(4,128)} %get-tuple-element.199) | copy-start | bytes 184324
  156.1 2.4 copy-start.29
  156.1 2.4 copy-start.13
  156.1 2.4 copy-start.32
  156.1 2.4 copy-start.33
  158.9 9.1 %copy-start.23 = (f32[128,64]{0,1:T(8,128)S(1)}, f32[128,64]{0,1:T(8,128)}, u32[]{:S(2)}) copy-start(f32[128,64]{0,1:T(8,128)} %fusion.20) | copy-start | bytes 98308
  169.1 103.5 %reduce-scatter.3.cloned.1.call-start = ((), (), s32[]{:S(2)}) async-start(), calls=%async_computation.2 | async-start | bytes 294912 | tf_op jit(solution)/shard_map/reduce_scatter | solution.py:197
  223.3 14.2 %copy-start.24 = (f32[128,64]{0,1:T(8,128)S(1)}, f32[128,64]{0,1:T(8,128)}, u32[]{:S(2)}) copy-start(f32[128,64]{0,1:T(8,128)} %fusion.26) | copy-start | bytes 98308
  223.3 49.3 %copy-start.16 = (bf16[64,5120]{1,0:T(8,128)(2,1)S(1)}, bf16[64,5120]{1,0:T(8,128)(2,1)}, u32[]{:S(2)}) copy-start(bf16[64,5120]{1,0:T(8,128)(2,1)} %param.43) | copy-start | bytes 1966084
  223.3 49.3 %copy-start.22 = (f32[64,128]{1,0:T(8,128)S(1)}, f32[64,128]{1,0:T(8,128)}, u32[]{:S(2)}) copy-start(f32[64,128]{1,0:T(8,128)} %get-tuple-element.231) | copy-start | bytes 98308
  238.6 171.7 %all-reduce.6.cloned.1.call-start = ((), (), s32[]{:S(2)}) async-start(), calls=%async_computation.4 | async-start | bytes 2621440 | tf_op jit(solution)/shard_map/psum | solution.py:215
  (18 other events, 25.7 us)
Sparse Core Ops, SparseCore 0:
  92.6 52.1 all-reduce.7
  169.2 34.3 reduce-scatter.4
  238.7 33.7 reduce-scatter.2
  278.4 131.9 all-reduce.5
where the time goes:
time: 421 us; the launch traced here: 419 us
  waiting for transfers between devices  224 us (53%)
  blocking collectives  82.3 us (20%)
  matrix products  55.5 us (13%)
  local copies, waits for them, and re-layouts  17.6 us (4%)
  between operations  15.8 us (4%)
  other arithmetic  13.9 us (3%)
  loops' own time  7.68 us (2%)
    psum x1, waiting for transfers between devices, per_device(): lax.psum(partial_grad / normalizer / grad_root, ('tm', 'batch'))  132 us
    reduce_scatter x1, waiting for transfers between devices, per_device(): lax.psum_scatter(term_fake, 'tm', scatter_dimension=1, tiled=True)  33.3 us
    psum x1, waiting for transfers between devices, per_device(): lax.psum((jnp.sum(qkv_real[0] * qkv_real[0], axis=1), jnp.sum(qkv_real[1]...  33.1 us
    psum x1, blocking collectives, per_device(): modul_real, modul_fake = lax.psum((share_real, share_fake), 'tm')  25.7 us
    reduce_scatter x1, waiting for transfers between devices, per_device(): lax.psum_scatter(term_real, 'tm', scatter_dimension=1, tiled=True)  25.1 us
    psum x1, blocking collectives, per_device(): lax.psum((jnp.sum(qkv_real[0] * qkv_real[0], axis=1), jnp.sum(qkv_real[1]...  13.3 us
    all_gather x1, blocking collectives, per_device(): lax.all_gather(noisy_patch.astype(jnp.float32), 'tm', axis=1, tiled=True)  10.2 us
    dot_general x6, matrix products, fold_one(): main_part = jnp.dot(widened, wide_weight, precision=highest)  9.04 us
  transfers between devices with their start and end apart: 5, of which 4 were waited for; matrix products, arithmetic and copies ran while one was open for 8% of the time, Pallas kernels for 0%

commit v1 on v0

--- a/solution.py
+++ b/solution.py
@@ -212,7 +212,9 @@
     partial_grad = jnp.dot(difference, hidden_states[0], preferred_element_type=jnp.float32)
     gap_total = lax.psum(gap_local, "tm")
     normalizer = jnp.maximum(gap_total / count_all, gap_floor)
-    weight_grad = lax.psum(partial_grad / normalizer / grad_root, ("tm", "batch"))
+    part = partial_grad / normalizer / grad_root
+    parts = lax.all_gather(part, ("tm", "batch"), axis=0, tiled=False)
+    weight_grad = parts.sum(axis=0)
     dmd_gradient = (gap_diff / normalizer)[None]
     return (dmd_gradient, weight_grad)
 

time: 421 us -> 531 us (1.26)
  waiting for transfers between devices: 224 us -> 325 us
  other arithmetic: 13.9 us -> 27.9 us
  local copies, waits for them, and re-layouts: 17.6 us -> 12 us
    all_gather x0 -> x1, waiting for transfers between devices: none -> 234 us  [per_device(): parts = lax.all_gather(part, ('tm', 'batch'), axis=0, tiled=False)]
    psum x1 -> x0, waiting for transfers between devices: 132 us -> none  [per_device(): lax.psum(partial_grad / normalizer / grad_root, ('tm', 'batch'))]
    reduce_sum x0 -> x1, other arithmetic: none -> 15.7 us  [per_device(): weight_grad = parts.sum(axis=0)]
  transfers between devices with their start and end apart: 5 -> 5, of which waited for: 4 -> 4; matrix products, arithmetic and copies ran while one was open for 8% -> 6% of each run, Pallas kernels for 0% -> 0%
where the time goes in v1:
time: 531 us; the launch traced here: 530 us
  waiting for transfers between devices  325 us (61%)
  blocking collectives  81.9 us (15%)
  matrix products  55.9 us (11%)
  other arithmetic  27.9 us (5%)
  between operations  15.8 us (3%)
  local copies, waits for them, and re-layouts  12 us (2%)
  loops' own time  7.32 us (1%)
    all_gather x1, waiting for transfers between devices, per_device(): parts = lax.all_gather(part, ('tm', 'batch'), axis=0, tiled=False)  234 us
    reduce_scatter x1, waiting for transfers between devices, per_device(): lax.psum_scatter(term_fake, 'tm', scatter_dimension=1, tiled=True)  33.2 us
    psum x1, waiting for transfers between devices, per_device(): lax.psum((jnp.sum(qkv_real[0] * qkv_real[0], axis=1), jnp.sum(qkv_real[1]...  33.1 us
    psum x1, blocking collectives, per_device(): modul_real, modul_fake = lax.psum((share_real, share_fake), 'tm')  25.3 us
    reduce_scatter x1, waiting for transfers between devices, per_device(): lax.psum_scatter(term_real, 'tm', scatter_dimension=1, tiled=True)  25.1 us
    reduce_sum x1, other arithmetic, per_device(): weight_grad = parts.sum(axis=0)  15.7 us
    psum x1, blocking collectives, per_device(): lax.psum((jnp.sum(qkv_real[0] * qkv_real[0], axis=1), jnp.sum(qkv_real[1]...  13.3 us
  transfers between devices with their start and end apart: 5, of which 4 were waited for; matrix products, arithmetic and copies ran while one was open for 6% of the time, Pallas kernels for 0%

profile of v1, /device:TPU:0, one launch (start us, length us, event | category | flops | bytes accessed | tf_op | source)
XLA Modules:
  0.0 529.6 jit_solution(6165187895158613940)
XLA Ops:
  8.5 2.3 fusion.74
  10.8 3.0 collective-permute-start
  15.8 25.3 %psum.52 = f32[3,5120]{1,0:T(4,128)S(1)} all-reduce(f32[3,5120]{1,0:T(4,128)S(1)} %bitcast.298), channel_id=1, replica_groups=mesh['tm'=8,'batch'=4] {'tm'}, use_global_device_ids=true, to_apply=%region_12.0 | all-reduce | flops 15360 | bytes 122880 | tf_op jit(solution)/shard_map/psum | solution.py:145
  43.0 1.9 fusion.97
  54.4 2.4 fusion.20
  56.8 10.2 %all_gather.22 = bf16[64,1024]{1,0:T(8,128)(2,1)S(1)} all-gather(bf16[64,128]{1,0:T(8,128)(2,1)S(1)} %get-tuple-element.224), channel_id=1, replica_groups=mesh['tm'=8,'batch'=4] {'tm'}, dimensions={1}, use_global_device_ids=true | all-gather | bytes 147456 | tf_op jit(solution)/shard_map/all_gather | solution.py:156
  68.8 7.6 %all-gather.3 = f32[8,1,128]{2,1,0:T(1,128)S(1)} all-gather(f32[1,1,128]{2,1,0:T(1,128)S(1)} %rsqrt_bitcast_fusion), channel_id=1, replica_groups=mesh['tm'=8,'batch'=4] {'tm'}, dimensions={0}, use_global_device_ids=true | all-gather | bytes 4608 | tf_op jit(solution)/shard_map/all_gather | solution.py:158
  76.5 9.0 %all-gather.4 = f32[8,1,128]{2,1,0:T(1,128)S(1)} all-gather(f32[1,1,128]{2,1,0:T(1,128)S(1)} %get-tuple-element.222), channel_id=1, replica_groups=mesh['tm'=8,'batch'=4] {'tm'}, dimensions={0}, use_global_device_ids=true | all-gather | bytes 4608 | tf_op jit(solution)/shard_map/all_gather | solution.py:157
  93.5 7.9 %all-gather.1 = f32[8,1,128]{2,1,0:T(1,128)S(1)} all-gather(f32[1,1,128]{2,1,0:T(1,128)} %rsqrt_bitcast_fusion.1), channel_id=1, replica_groups=mesh['tm'=8,'batch'=4] {'tm'}, dimensions={0}, use_global_device_ids=true | all-gather | bytes 4608 | tf_op jit(solution)/shard_map/all_gather | solution.py:160
  101.4 8.7 %all-gather.2 = f32[8,1,128]{2,1,0:T(1,128)S(1)} all-gather(f32[1,1,128]{2,1,0:T(1,128)} %get-tuple-element.220), channel_id=1, replica_groups=mesh['tm'=8,'batch'=4] {'tm'}, dimensions={0}, use_global_device_ids=true | all-gather | bytes 4608 | tf_op jit(solution)/shard_map/all_gather | solution.py:159
  110.7 33.1 %all-reduce.5.cloned.1.call-done = (f32[1024]{0:T(1024)}, f32[1024]{0:T(1024)}, f32[3,5120]{1,0:T(4,128)}) async-done(((f32[1024]{0:T(1024)}, f32[1024]{0:T(1024)}, f32[3,5120]{1,0:T(4,128)}), (f32[1024]{0:T(1024)}, f32[1024]{0:T(1024)}, f32[3,5120]{1,0:T(4,128)})) %all-reduce.5.cloned.1.call-update) | async-done | bytes 69648 | tf_op jit(solution)/shard_map/psum | solution.py:173
  143.8 2.1 fusion.85
  145.9 2.0 fusion.94
  158.2 9.1 %while.23 = (s32[]{:T(128)}, bf16[2,512,1,128]{3,1,2,0:T(8,128)(2,1)S(1)}, s32[1024]{0:T(1024)S(1)}, s32[2]{0:T(128)S(1)}, bf16[1024,1,128]{0,2,1:T(8,128)(2,1)S...) while((s32[]{:T(128)}, ...), condition=%wide.region_22.23_spmd.clone, body=%wide.region_19.22_spmd.clone.sunk | while | flops 273218560 | bytes 7098535 | solution.py:91
  168.6 2.1 fusion.30
  173.9 3.9 fusion.26
  177.8 25.1 %reduce-scatter.5.cloned.1.call-done = f32[64,128]{1,0:T(8,128)} async-done(((f32[64,1024]{1,0:T(8,128)}), f32[64,128]{1,0:T(8,128)}) %reduce-scatter.5.cloned.1.call-update) | async-done | bytes 32784 | tf_op jit(solution)/shard_map/reduce_scatter | solution.py:196
  202.9 4.6 abs_reduce_fusion
  207.5 13.3 %all-reduce.1 = (f32[1024]{0:T(1024)S(1)}, f32[1024]{0:T(1024)S(1)}, f32[]{:T(128)}) all-reduce(f32[1024]{0:T(1024)} %get-tuple-element.163, f32[1024]{0:T(1024)} %get-tuple-element.162, f32[]{:T(128)} %get-tuple-element.230), channel_id=1, replica_groups=mesh['tm'=8,'batch'=4] {'tm'}, use_global_device_ids=true, to_apply=%region_4.0 | all-reduce | flops 2049 | bytes 16392 | tf_op jit(solution)/shard_map/psum | solution.py:173
  222.6 10.4 %while.22 = (s32[]{:T(128)}, bf16[2,512,1,128]{3,1,2,0:T(8,128)(2,1)S(1)}, s32[1024]{0:T(1024)S(1)}, s32[2]{0:T(128)S(1)}, bf16[1024,1,128]{0,2,1:T(8,128)(2,1)}...) while((s32[]{:T(128)}, ...), condition=%wide.region_10.0_spmd.clone, body=%wide.region_7.10_spmd.clone.sunk | while | flops 273218560 | bytes 7098535 | solution.py:91
  234.8 33.2 %reduce-scatter.3.cloned.1.call-done = f32[64,128]{1,0:T(8,128)} async-done(((f32[64,1024]{1,0:T(8,128)}), f32[64,128]{1,0:T(8,128)}) %reduce-scatter.3.cloned.1.call-update) | async-done | bytes 32784 | tf_op jit(solution)/shard_map/reduce_scatter | solution.py:197
  268.0 3.4 fusion.46
  273.4 234.0 %all-gather.7.cloned.1.call-done = f32[2048,5120]{1,0:T(8,128)} async-done(((f32[64,5120]{1,0:T(8,128)}), f32[2048,5120]{1,0:T(8,128)}) %all-gather.7.cloned.1.call-update) | async-done | bytes 41943056 | tf_op jit(solution)/shard_map/all_gather | solution.py:216
  507.4 15.7 %reduce_sum.117 = f32[64,5120]{1,0:T(8,128)} reduce(f32[32,64,5120]{2,1,0:T(8,128)} %bitcast.288, f32[]{:T(128)} %constant.103.clone.1), dimensions={0}, to_apply=%region_26.27 | reduce | flops 10158080 | bytes 43253764 | tf_op jit(solution)/shard_map/reduce_sum | solution.py:217
  (180 shorter events, 55.9 us)
Async XLA Ops:
  7.2 8.3 %copy-start.17 = (bf16[32,3,5120]{2,0,1:T(8,128)(2,1)S(1)}, bf16[32,3,5120]{2,0,1:T(8,128)(2,1)}, u32[]{:S(2)}) copy-start(bf16[32,3,5120]{2,0,1:T(8,128)(2,1)} %param.29) | copy-start | bytes 2949124
  7.2 136.6 %all-reduce.5.cloned.1.call-start = ((), (), s32[]{:S(2)}) async-start(), calls=%async_computation.5 | async-start | bytes 180224 | tf_op jit(solution)/shard_map/psum | solution.py:173
  10.8 56.3 %collective-permute-start = (bf16[64,128]{1,0:T(8,128)(2,1)S(1)}, bf16[64,128]{1,0:T(8,128)(2,1)}, u32[]{:S(2)}, u32[]{:S(2)}) collective-permute-start(bf16[64,128]{1,0:T(8,128)(2,1)S(1)} %get-tuple-element.224), channel_id=1, source_target_pairs={{0,4},{4,8},{8,12},{12,16},{16,20},{20,24},{24,28},{1,5},{5,9},{9,... | collective-permute-start | bytes 49160 | tf_op jit(solution)/shard_map/ppermute | solution.py:18
  15.8 29.2 %copy-start.5 = (bf16[5120,128]{1,0:T(8,128)(2,1)S(1)}, bf16[5120,128]{1,0:T(8,128)(2,1)}, u32[]{:S(2)}) copy-start(bf16[5120,128]{1,0:T(8,128)(2,1)} %param.32) | copy-start | bytes 3932164
  50.6 2.8 copy-start.18
  67.0 18.4 %copy-start.19 = (bf16[64,1024]{1,0:T(8,128)(2,1)}, bf16[64,1024]{1,0:T(8,128)(2,1)S(1)}, u32[]{:S(2)}) copy-start(bf16[64,1024]{1,0:T(8,128)(2,1)S(1)} %all_gather.22) | copy-start | bytes 393220
  67.0 18.4 %copy-start.27 = (bf16[64,896]{1,0:T(8,128)(2,1)}, bf16[64,896]{1,0:T(8,128)(2,1)S(1)}, u32[]{:S(2)}) copy-start(bf16[64,896]{1,0:T(8,128)(2,1)S(1)} %slice.122) | copy-start | bytes 344068
  68.4 18.0 %copy-start.2 = (f32[128,5120]{1,0:T(8,128)}, f32[128,5120]{1,0:T(8,128)S(1)}, u32[]{:S(2)}) copy-start(f32[128,5120]{1,0:T(8,128)S(1)} %get-tuple-element.227) | copy-start | bytes 7864324
  91.4 111.4 %reduce-scatter.5.cloned.1.call-start = ((), (), s32[]{:S(2)}) async-start(), calls=%async_computation.3 | async-start | bytes 294912 | tf_op jit(solution)/shard_map/reduce_scatter | solution.py:196
  101.4 47.1 %copy-start.28 = (f32[8,1,128]{2,1,0:T(1,128)}, f32[8,1,128]{2,1,0:T(1,128)S(1)}, u32[]{:S(2)}) copy-start(f32[8,1,128]{2,1,0:T(1,128)S(1)} %all-gather.1) | copy-start | bytes 12292
  143.8 4.1 copy-start.8
  143.8 4.1 copy-start.13
  154.2 3.6 copy-start.12
  154.2 3.5 copy-start.33
  154.2 3.5 copy-start.34
  158.1 9.1 %copy-start.25 = (f32[128,64]{0,1:T(8,128)S(1)}, f32[128,64]{0,1:T(8,128)}, u32[]{:S(2)}) copy-start(f32[128,64]{0,1:T(8,128)} %fusion.20) | copy-start | bytes 98308
  168.3 99.6 %reduce-scatter.3.cloned.1.call-start = ((), (), s32[]{:S(2)}) async-start(), calls=%async_computation.2 | async-start | bytes 294912 | tf_op jit(solution)/shard_map/reduce_scatter | solution.py:197
  207.5 15.0 %copy-start.21 = (bf16[1024,1,128]{2,0,1:T(8,128)(2,1)S(1)}, bf16[1024,1,128]{2,0,1:T(8,128)(2,1)}, u32[]{:S(2)}) copy-start(bf16[1024,1,128]{2,0,1:T(8,128)(2,1)} %copy.41) | copy-start | bytes 786436
  207.5 15.0 %copy-start.23 = (s32[1024]{0:T(1024)S(1)}, s32[1024]{0:T(1024)}, u32[]{:S(2)}) copy-start(s32[1024]{0:T(1024)} %add_select_fusion) | copy-start | bytes 12292
  207.5 15.0 %copy-start.38 = (s32[2]{0:T(128)S(1)}, s32[2]{0:T(128)}, u32[]{:S(2)}) copy-start(s32[2]{0:T(128)} %iota_multiply_fusion) | copy-start | bytes 28
  222.6 10.4 %copy-start.26 = (f32[128,64]{0,1:T(8,128)S(1)}, f32[128,64]{0,1:T(8,128)}, u32[]{:S(2)}) copy-start(f32[128,64]{0,1:T(8,128)} %fusion.26) | copy-start | bytes 98308
  222.6 45.4 %copy-start.15 = (bf16[64,5120]{1,0:T(8,128)(2,1)S(1)}, bf16[64,5120]{1,0:T(8,128)(2,1)}, u32[]{:S(2)}) copy-start(bf16[64,5120]{1,0:T(8,128)(2,1)} %param.43) | copy-start | bytes 1966084
  222.6 45.4 %copy-start.24 = (f32[64,128]{1,0:T(8,128)S(1)}, f32[64,128]{1,0:T(8,128)}, u32[]{:S(2)}) copy-start(f32[64,128]{1,0:T(8,128)} %get-tuple-element.231) | copy-start | bytes 98308
  234.1 273.3 %all-gather.7.cloned.1.call-start = ((), (), s32[]{:S(2)}) async-start(), calls=%async_computation.4 | async-start | bytes 43253760 | tf_op jit(solution)/shard_map/all_gather | solution.py:216
  (20 other events, 37.4 us)
Sparse Core Ops, SparseCore 0:
  91.6 52.2 all-reduce.4
  168.5 34.3 reduce-scatter.4
  234.2 33.6 reduce-scatter.2
  272.9 234.4 all-gather.6
